TPU v7x, 32 devices: a whole 2x2x4 slice. The times are simulated.
32 devices in a mesh: row: 16 (over z, y, core), col: 2 (over x).
Axes of the slice: x: 2, y: 2, z: 4, core: 2. Of those that a mesh axis runs over, the one named last changes fastest.
Arguments:
- eigvec: float32 [65536, 1024], P('row', 'col'), may hold values from -6 to 6
- reflectors: float32 [16, 2, 1024, 256], P('row', 'col'), may hold values from -0.125 to 0.125
- tfactors: float32 [16, 2, 256, 256], P('row', 'col'), may hold values from -1 to 1, as said below
- offsets: int32 [2, 16], replicated, may hold values from 3072 to 3584
- owners: int32 [2, 16], replicated, may hold values from 0 to 1
Outputs:
- result: float32 [65536, 1024], P('row', 'col')
Inputs may be any that keep to these rules, and one draw needn't show every extreme that they name: `tfactors`: every factor block is zero below its diagonal.
All inputs are finite; a program needn't handle non-finite values.
Results may differ from a plain program's by a relative error of at most 0.0003.
Values sent between devices are 32-bit elements; how exact they have to be, the bound alone decides.
A program may use at most 64 MiB of HBM per device.

v0:
```python
import jax
import jax.numpy as jnp
from jax import lax
from jax.sharding import PartitionSpec as P

WIN = 1024
TICKS = 2


def from_root(block, axis, owner):
    block = jnp.where(lax.axis_index(axis) == owner, block, jnp.zeros_like(block))
    return lax.psum(block, axis)


def from_behind(shard, axis, by):
    count = lax.axis_size(axis)
    pairs = [(i, i + by) for i in range(count) if 0 <= i + by < count]
    return lax.ppermute(shard, axis, pairs)


def project(vectors, window):
    return lax.dot_general(
        vectors,
        window,
        (((0,), (0,)), ((), ())),
        precision=lax.Precision.HIGHEST,
        preferred_element_type=jnp.float32,
    )


def product(left, right):
    return jnp.dot(left, right, precision=lax.Precision.HIGHEST, preferred_element_type=jnp.float32)


def per_device(eigvec, reflectors, tfactors, offsets, owners):
    row_count = eigvec.shape[0]
    half_rows = WIN // 2
    own_row = lax.axis_index("row")
    vector_local = reflectors[0, 0]
    factor_local = tfactors[0, 0]
    lower_rows = from_behind(eigvec[:half_rows], "row", -1)
    extended = jnp.concatenate([eigvec, lower_rows], 0)
    for turn_index in range(TICKS):
        source = owners[turn_index, own_row]
        begin_row = offsets[turn_index, own_row]
        window = lax.dynamic_slice_in_dim(extended, begin_row, WIN, 0)
        vector_block = from_root(vector_local, "col", source)
        other_block = from_root(factor_local, "col", source)
        coefficients = project(vector_block, window)
        window = window - product(vector_block, product(other_block, coefficients))
        extended = lax.dynamic_update_slice_in_dim(extended, window, begin_row, 0)
    upper_rows = from_behind(extended[row_count:], "row", 1)
    top_rows = jnp.where(own_row > 0, upper_rows, extended[:half_rows])
    return jnp.concatenate([top_rows, extended[half_rows:row_count]], 0)


def solution(mesh):
    return jax.shard_map(
        per_device,
        mesh=mesh,
        in_specs=(
            P("row", "col"),
            P("row", "col", None, None),
            P("row", "col", None, None),
            P(),
            P(),
        ),
        out_specs=P("row", "col"),
        check_vma=False,
    )
```

profile of v0, /device:TPU:16, one launch (start us, length us, event | category | flops | bytes accessed | tf_op | source)
XLA Modules:
  0.0 150.8 jit_solution(7027749103018605000)
XLA Ops:
  6.5 1.4 constant_dynamic-slice_fusion.2
  9.2 2.7 %select_bitcast_fusion = (f32[1024,256]{1,0:T(8,128)}, f32[1024,256]{1,0:T(8,128)}) fusion(f32[1,1,1024,256]{3,2,1,0:T(8,128)} %param.6, pred[]{:T(512)S(6)} %eq.9, pred[]{:T(512)S(6)} %eq.8), kind=kLoop, calls=%fused_computation.8 | loop fusion | flops 524288 | bytes 3145730 | tf_op jit(solution)/shard_map/jit(_where)/select_n | solution.py:11
  11.9 1.8 %select_bitcast_fusion.2 = (f32[256,256]{1,0:T(8,128)}, f32[256,256]{1,0:T(8,128)}) fusion(f32[1,1,256,256]{3,2,1,0:T(8,128)} %param.7, pred[]{:T(512)S(6)} %eq.9, pred[]{:T(512)S(6)} %eq.8), kind=kLoop, calls=%fused_computation.10 | loop fusion | flops 131072 | bytes 786434 | tf_op jit(solution)/shard_map/jit(_where)/select_n | solution.py:11
  13.7 0.0 all-reduce.3.cloned.1.call-update
  13.8 1.3 slice.12
  15.1 2.8 %collective-permute-start = (f32[512,512]{1,0:T(8,128)S(1)}, f32[512,512]{1,0:T(8,128)S(1)}, u32[]{:S(2)}, u32[]{:S(2)}) collective-permute-start(f32[512,512]{1,0:T(8,128)S(1)} %slice.12), channel_id=1, source_target_pairs={{2,0},{4,2},{6,4},{8,6},{10,8},{12,10},{14,12},{16,14},{18,16},{20... | collective-permute-start | bytes 3145736 | tf_op jit(solution)/shard_map/ppermute | solution.py:18
  21.6 7.6 %constant_dynamic-update-slice_fusion.1 = f32[4608,512]{1,0:T(8,128)} fusion(f32[4096,512]{1,0:T(8,128)} %param.5), kind=kLoop, calls=%fused_computation.13 | loop fusion | bytes 16777216
  29.2 0.9 collective-permute-done
  30.1 1.1 constant_dynamic-update-slice_fusion
  31.2 58.2 %all-reduce.3.cloned.1.call-done = (f32[1024,256]{1,0:T(8,128)}, f32[256,256]{1,0:T(8,128)}, f32[1024,256]{1,0:T(8,128)}, f32[256,256]{1,0:T(8,128)}) async-done(((f32[1024,256]{1,0:T(8,128)}, f32[256,256]{1,0:T(8,128)}, f32[1024,256]{1,0:T(8,128)}, f32[256,256]{1,0:T(8,128)}), (f32[1024,256]{1,0:T(8,128)}, f32[256,256]{1,0:T(8,128)}, f32[1024,256]{1,0:T(8,128)}, ...) | async-done | bytes 2621456 | tf_op jit(solution)/shard_map/psum | solution.py:12
  89.4 4.0 %fusion.2 = f32[256,512]{1,0:T(8,128)S(1)} fusion(f32[1024,256]{1,0:T(8,128)} %get-tuple-element.5, f32[4608,512]{1,0:T(8,128)} %constant_dynamic-update-slice_fusion, s32[]{:T(128)S(6)} %select_n.64), kind=kOutput, calls=%fused_computation.5 | convolution fusion | flops 1610612736 | bytes 3670020 | tf_op jit(solution)/shard_map/dot_general | solution.py:22
  93.5 1.6 %fusion.6 = f32[256,512]{1,0:T(8,128)S(1)} fusion(f32[256,256]{1,0:T(8,128)} %get-tuple-element.6, f32[256,512]{1,0:T(8,128)S(1)} %fusion.2), kind=kOutput, calls=%fused_computation.20 | convolution fusion | flops 402653184 | bytes 1310720 | tf_op jit(solution)/shard_map/dot_general | solution.py:32
  95.1 3.9 %dynamic-slice_subtract_fusion.1 = f32[1024,512]{1,0:T(8,128)S(1)} fusion(f32[4608,512]{1,0:T(8,128)} %constant_dynamic-update-slice_fusion, s32[]{:T(128)S(6)} %select_n.64, f32[1024,256]{1,0:T(8,128)} %get-tuple-element.5, f32[256,512]{1,0:T(8,128)S(1)} %fusion.6), kind=kOutput, calls=%fused_computation.4 | convolution fusion | flops 1611137024 | bytes 5767172 | tf_op jit(solution)/shard_map/dot_general | solution.py:32
  99.0 6.5 %dynamic_update_slice.6 = f32[4608,512]{1,0:T(8,128)} dynamic-update-slice(f32[4608,512]{1,0:T(8,128)} %constant_dynamic-update-slice_fusion, f32[1024,512]{1,0:T(8,128)S(1)} %dynamic-slice_subtract_fusion.1, s32[]{:T(128)S(6)} %select_n.64, s32[]{:T(128)} %constant.3.clone.1) | dynamic-update-slice | bytes 4194308 | tf_op jit(solution)/shard_map/dynamic_update_slice | solution.py:51
  105.5 3.6 %fusion = f32[256,512]{1,0:T(8,128)S(1)} fusion(f32[1024,256]{1,0:T(8,128)S(1)} %copy-done, f32[4608,512]{1,0:T(8,128)} %dynamic_update_slice.6, s32[]{:T(128)S(6)} %select_n.71), kind=kOutput, calls=%fused_computation.2 | convolution fusion | flops 1610612736 | bytes 3670020 | tf_op jit(solution)/shard_map/dot_general | solution.py:22
  109.1 0.6 fusion.7
  109.8 3.5 %dynamic-slice_subtract_fusion = f32[1024,512]{1,0:T(8,128)S(1)} fusion(f32[4608,512]{1,0:T(8,128)} %dynamic_update_slice.6, s32[]{:T(128)S(6)} %select_n.71, f32[1024,256]{1,0:T(8,128)S(1)} %copy-done, f32[256,512]{1,0:T(8,128)S(1)} %fusion.7), kind=kOutput, calls=%fused_computation.1 | convolution fusion | flops 1611137024 | bytes 5767172 | tf_op jit(solution)/shard_map/dot_general | solution.py:32
  113.3 6.5 %dynamic_update_slice.7 = f32[4608,512]{1,0:T(8,128)} dynamic-update-slice(f32[4608,512]{1,0:T(8,128)} %dynamic_update_slice.6, f32[1024,512]{1,0:T(8,128)S(1)} %dynamic-slice_subtract_fusion, s32[]{:T(128)S(6)} %select_n.71, s32[]{:T(128)} %constant.3.clone.1) | dynamic-update-slice | bytes 4194308 | tf_op jit(solution)/shard_map/dynamic_update_slice | solution.py:51
  119.8 1.3 slice.16
  121.1 1.9 %collective-permute-start.1 = (f32[512,512]{1,0:T(8,128)S(1)}, f32[512,512]{1,0:T(8,128)S(1)}, u32[]{:S(2)}, u32[]{:S(2)}) collective-permute-start(f32[512,512]{1,0:T(8,128)S(1)} %slice.16), channel_id=1, source_target_pairs={{0,2},{2,4},{4,6},{6,8},{8,10},{10,12},{12,14},{14,16},{16,18},{18... | collective-permute-start | bytes 3145736 | tf_op jit(solution)/shard_map/ppermute | solution.py:18
  123.1 3.9 %slice.18 = f32[3584,512]{1,0:T(8,128)S(1)} slice(f32[4608,512]{1,0:T(8,128)} %dynamic_update_slice.7), slice={[512:4096], [0:512]} | slice | bytes 14680064 | tf_op jit(solution)/shard_map/slice | solution.py:54
  127.0 11.2 %collective-permute-done.1 = f32[512,512]{1,0:T(8,128)S(1)} collective-permute-done((f32[512,512]{1,0:T(8,128)S(1)}, f32[512,512]{1,0:T(8,128)S(1)}, u32[]{:S(2)}, u32[]{:S(2)}) %collective-permute-start.1) | collective-permute-done | bytes 1048608 | tf_op jit(solution)/shard_map/ppermute | solution.py:18
  138.1 1.4 slice_select_fusion
  139.6 4.4 %pad_maximum_fusion = f32[4096,512]{1,0:T(8,128)} fusion(f32[3584,512]{1,0:T(8,128)S(1)} %slice.18, f32[512,512]{1,0:T(8,128)S(1)} %slice_select_fusion), kind=kLoop, calls=%fused_computation | loop fusion | flops 2097152 | bytes 16777216 | tf_op jit(solution)/shard_map/concatenate | solution.py:54
  (5 shorter events, 0.0 us)
Async XLA Ops:
  6.5 82.9 %all-reduce.3.cloned.1.call-start = ((), (), s32[]{:S(2)}) async-start(), calls=%async_computation | async-start | bytes 5242880 | tf_op jit(solution)/shard_map/psum | solution.py:12
  15.1 15.1 %collective-permute-start = (f32[512,512]{1,0:T(8,128)S(1)}, f32[512,512]{1,0:T(8,128)S(1)}, u32[]{:S(2)}, u32[]{:S(2)}) collective-permute-start(f32[512,512]{1,0:T(8,128)S(1)} %slice.12), channel_id=1, source_target_pairs={{2,0},{4,2},{6,4},{8,6},{10,8},{12,10},{14,12},{16,14},{18,16},{20... | collective-permute-start | bytes 3145736 | tf_op jit(solution)/shard_map/ppermute | solution.py:18
  89.4 16.1 %copy-start = (f32[1024,256]{1,0:T(8,128)S(1)}, f32[1024,256]{1,0:T(8,128)}, u32[]{:S(2)}) copy-start(f32[1024,256]{1,0:T(8,128)} %get-tuple-element.7) | copy-start | bytes 3145732
  93.5 15.7 %copy-start.1 = (f32[256,256]{1,0:T(8,128)S(1)}, f32[256,256]{1,0:T(8,128)}, u32[]{:S(2)}) copy-start(f32[256,256]{1,0:T(8,128)} %get-tuple-element.8) | copy-start | bytes 786436
  121.1 17.0 %collective-permute-start.1 = (f32[512,512]{1,0:T(8,128)S(1)}, f32[512,512]{1,0:T(8,128)S(1)}, u32[]{:S(2)}, u32[]{:S(2)}) collective-permute-start(f32[512,512]{1,0:T(8,128)S(1)} %slice.16), channel_id=1, source_target_pairs={{0,2},{2,4},{4,6},{6,8},{8,10},{10,12},{12,14},{14,16},{16,18},{18... | collective-permute-start | bytes 3145736 | tf_op jit(solution)/shard_map/ppermute | solution.py:18
Sparse Core Ops, SparseCore 0:
  13.9 75.4 all-reduce.2
where the time goes:
time: 152 us; the launch traced here: 151 us
  waiting for transfers between devices  70.2 us (46%)
  local copies, waits for them, and re-layouts  29.7 us (20%)
  between operations  18.5 us (12%)
  matrix products  17.3 us (11%)
  other arithmetic  10.3 us (7%)
  starting transfers between devices  4.68 us (3%)
    psum x1, waiting for transfers between devices, from_root(): return lax.psum(block, axis)  58.2 us
    dynamic_update_slice x2, local copies, waits for them, and re-layouts, per_device(): extended = lax.dynamic_update_slice_in_dim(extended, window, begin_row, 0)  13 us
    ppermute x2, waiting for transfers between devices, from_behind(): return lax.ppermute(shard, axis, pairs)  12 us
    dot_general x4, matrix products, product(): jnp.dot(left, right, precision=lax.Precision.HIGHEST, preferred_element_t...  9.63 us
    dot_general x2, matrix products, project(): lax.dot_general(vectors, window, (((0,), (0,)), ((), ())), precision=lax....  7.68 us
    unnamed x5, local copies, waits for them, and re-layouts  7.65 us
    ppermute x2, starting transfers between devices, from_behind(): return lax.ppermute(shard, axis, pairs)  4.67 us
    select_n x2, other arithmetic, from_root(): jnp.where(lax.axis_index(axis) == owner, block, jnp.zeros_like(block))  4.52 us
  transfers between devices with their start and end apart: 3, of which 3 were waited for; matrix products, arithmetic and copies ran while one was open for 9% of the time, Pallas kernels for 0%

commit v1 on v0

--- a/solution.py
+++ b/solution.py
@@ -9,7 +9,7 @@
 
 def from_root(block, axis, owner):
     block = jnp.where(lax.axis_index(axis) == owner, block, jnp.zeros_like(block))
-    return lax.psum(block, axis)
+    return jnp.sum(lax.all_gather(block, axis), axis=0)
 
 
 def from_behind(shard, axis, by):

time: 152 us -> 140 us (0.921)
  waiting for transfers between devices: 70.2 us -> 28.2 us
  blocking collectives: 0 us -> 29.1 us
  other arithmetic: 10.3 us -> 13.3 us
    psum x1 -> x0, waiting for transfers between devices: 58.2 us -> none  [from_root(): return lax.psum(block, axis)]
    all_gather x0 -> x2, blocking collectives: none -> 29.1 us  [from_root(): return jnp.sum(lax.all_gather(block, axis), axis=0)]
    all_gather x0 -> x2, waiting for transfers between devices: none -> 17 us  [from_root(): return jnp.sum(lax.all_gather(block, axis), axis=0)]
    reduce_sum x0 -> x4, other arithmetic: none -> 3.76 us  [from_root(): return jnp.sum(lax.all_gather(block, axis), axis=0)]
    unnamed x5 -> x1, local copies, waits for them, and re-layouts: 7.65 us -> 7.58 us
  transfers between devices with their start and end apart: 3 -> 4, of which waited for: 3 -> 2; matrix products, arithmetic and copies ran while one was open for 9% -> 23% of each run, Pallas kernels for 0% -> 0%
where the time goes in v1:
time: 140 us; the launch traced here: 139 us
  local copies, waits for them, and re-layouts  29.7 us (21%)
  blocking collectives  29.1 us (21%)
  waiting for transfers between devices  28.2 us (20%)
  between operations  18.5 us (13%)
  matrix products  15.8 us (11%)
  other arithmetic  13.3 us (10%)
  starting transfers between devices  4.72 us (3%)
    all_gather x2, blocking collectives, from_root(): return jnp.sum(lax.all_gather(block, axis), axis=0)  29.1 us
    all_gather x2, waiting for transfers between devices, from_root(): return jnp.sum(lax.all_gather(block, axis), axis=0)  17 us
    dynamic_update_slice x2, local copies, waits for them, and re-layouts, per_device(): extended = lax.dynamic_update_slice_in_dim(extended, window, begin_row, 0)  13.1 us
    ppermute x2, waiting for transfers between devices, from_behind(): return lax.ppermute(shard, axis, pairs)  11.2 us
    dot_general x4, matrix products, product(): jnp.dot(left, right, precision=lax.Precision.HIGHEST, preferred_element_t...  8.5 us
    unnamed x1, local copies, waits for them, and re-layouts  7.58 us
    dot_general x2, matrix products, project(): lax.dot_general(vectors, window, (((0,), (0,)), ((), ())), precision=lax....  7.3 us
    ppermute x2, starting transfers between devices, from_behind(): return lax.ppermute(shard, axis, pairs)  4.67 us
  transfers between devices with their start and end apart: 4, of which 2 were waited for; matrix products, arithmetic and copies ran while one was open for 23% of the time, Pallas kernels for 0%

profile of v1, /device:TPU:16, one launch (start us, length us, event | category | flops | bytes accessed | tf_op | source)
XLA Modules:
  0.0 139.4 jit_solution(4103102513965723903)
XLA Ops:
  6.5 1.4 %constant_dynamic-slice_fusion.2 = (s32[1,1]{1,0:T(1,128)}, s32[1,1]{1,0:T(1,128)}, s32[1,1]{1,0:T(1,128)}, s32[1,1]{1,0:T(1,128)}) fusion(s32[2,16]{1,0:T(2,128)} %param.9, s32[]{:T(128)S(6)} %select_n.91, s32[2,16]{1,0:T(2,128)} %param.8), kind=kLoop, calls=%fused_computation.18 | loop fusion | bytes 36 | tf_op jit(solution)/shard_map/dynamic_slice | solution.py:44
  9.3 2.7 %broadcast_select_fusion = (f32[1,1,1024,256]{3,2,1,0:T(8,128)}, f32[1,1,1024,256]{3,2,1,0:T(8,128)}) fusion(f32[1,1,1024,256]{3,2,1,0:T(8,128)} %param.6, pred[]{:T(512)S(6)} %eq.9, pred[]{:T(512)S(6)} %eq.8), kind=kLoop, calls=%fused_computation.8 | loop fusion | flops 524288 | bytes 3145730 | tf_op jit(solution)/shard_map/jit(_where)/select_n | solution.py:11
  12.0 1.3 slice.12
  13.3 2.8 %collective-permute-start = (f32[512,512]{1,0:T(8,128)S(1)}, f32[512,512]{1,0:T(8,128)S(1)}, u32[]{:S(2)}, u32[]{:S(2)}) collective-permute-start(f32[512,512]{1,0:T(8,128)S(1)} %slice.12), channel_id=1, source_target_pairs={{2,0},{4,2},{6,4},{8,6},{10,8},{12,10},{14,12},{16,14},{18,16},{20... | collective-permute-start | bytes 3145736 | tf_op jit(solution)/shard_map/ppermute | solution.py:18
  18.6 1.0 broadcast_select_fusion.2
  19.6 14.1 %all-gather.1 = f32[2,1,256,256]{3,2,1,0:T(8,128)S(1)} all-gather(f32[1,1,256,256]{3,2,1,0:T(8,128)S(1)} %get-tuple-element.8), channel_id=3, replica_groups=mesh['row'=16,'col'=2] {'col'}, dimensions={0}, use_global_device_ids=true | all-gather | bytes 786432 | tf_op jit(solution)/shard_map/all_gather | solution.py:12
  33.8 15.0 %all-gather.3 = f32[2,1,256,256]{3,2,1,0:T(8,128)S(1)} all-gather(f32[1,1,256,256]{3,2,1,0:T(8,128)S(1)} %get-tuple-element.7), channel_id=5, replica_groups=mesh['row'=16,'col'=2] {'col'}, dimensions={0}, use_global_device_ids=true | all-gather | bytes 786432 | tf_op jit(solution)/shard_map/all_gather | solution.py:12
  50.1 7.6 %constant_dynamic-update-slice_fusion.1 = f32[4608,512]{1,0:T(8,128)} fusion(f32[4096,512]{1,0:T(8,128)} %param.5), kind=kLoop, calls=%fused_computation.13 | loop fusion | bytes 16777216
  57.6 1.1 constant_dynamic-update-slice_fusion
  58.8 1.8 %reduce_sum.36 = f32[1024,256]{1,0:T(8,128)S(1)} reduce(f32[2,1,1024,256]{3,2,1,0:T(8,128)} %all-gather.7.cloned.1.call-done, f32[]{:T(128)} %constant.5.clone.1), dimensions={0,1}, to_apply=%region_0.1 | reduce | flops 262144 | bytes 3145732 | tf_op jit(solution)/shard_map/reduce_sum | solution.py:12
  60.6 3.7 %fusion.2 = f32[256,512]{1,0:T(8,128)S(1)} fusion(f32[1024,256]{1,0:T(8,128)S(1)} %reduce_sum.36, f32[4608,512]{1,0:T(8,128)} %constant_dynamic-update-slice_fusion, s32[]{:T(128)S(6)} %select_n.92), kind=kOutput, calls=%fused_computation.5 | convolution fusion | flops 1610612736 | bytes 3670020 | tf_op jit(solution)/shard_map/dot_general | solution.py:22
  64.9 3.7 %dynamic-slice_subtract_fusion.1 = f32[1024,512]{1,0:T(8,128)S(1)} fusion(f32[4608,512]{1,0:T(8,128)} %constant_dynamic-update-slice_fusion, s32[]{:T(128)S(6)} %select_n.92, f32[1024,256]{1,0:T(8,128)S(1)} %reduce_sum.36, f32[256,512]{1,0:T(8,128)S(1)} %fusion.6), kind=kOutput, calls=%fused_computation.4 | convolution fusion | flops 1611137024 | bytes 5767172 | tf_op jit(solution)/shard_map/dot_general | solution.py:32
  68.7 6.5 %dynamic_update_slice.6 = f32[4608,512]{1,0:T(8,128)} dynamic-update-slice(f32[4608,512]{1,0:T(8,128)} %constant_dynamic-update-slice_fusion, f32[1024,512]{1,0:T(8,128)S(1)} %dynamic-slice_subtract_fusion.1, s32[]{:T(128)S(6)} %select_n.92, s32[]{:T(128)} %constant.9.clone.1) | dynamic-update-slice | bytes 4194308 | tf_op jit(solution)/shard_map/dynamic_update_slice | solution.py:51
  75.2 17.0 %all-gather.9.cloned.1.call-done = f32[2,1,1024,256]{3,2,1,0:T(8,128)} async-done(((f32[1,1,1024,256]{3,2,1,0:T(8,128)}), f32[2,1,1024,256]{3,2,1,0:T(8,128)}) %all-gather.9.cloned.1.call-update) | async-done | bytes 2097168 | tf_op jit(solution)/shard_map/all_gather | solution.py:12
  92.2 1.8 %reduce_sum.38 = f32[1024,256]{1,0:T(8,128)S(1)} reduce(f32[2,1,1024,256]{3,2,1,0:T(8,128)} %all-gather.9.cloned.1.call-done, f32[]{:T(128)} %constant.5.clone.1), dimensions={0,1}, to_apply=%region_2.3 | reduce | flops 262144 | bytes 3145732 | tf_op jit(solution)/shard_map/reduce_sum | solution.py:12
  94.0 3.6 %fusion = f32[256,512]{1,0:T(8,128)S(1)} fusion(f32[1024,256]{1,0:T(8,128)S(1)} %reduce_sum.38, f32[4608,512]{1,0:T(8,128)} %dynamic_update_slice.6, s32[]{:T(128)S(6)} %select_n.99), kind=kOutput, calls=%fused_computation.2 | convolution fusion | flops 1610612736 | bytes 3670020 | tf_op jit(solution)/shard_map/dot_general | solution.py:22
  98.3 3.5 %dynamic-slice_subtract_fusion = f32[1024,512]{1,0:T(8,128)S(1)} fusion(f32[4608,512]{1,0:T(8,128)} %dynamic_update_slice.6, s32[]{:T(128)S(6)} %select_n.99, f32[1024,256]{1,0:T(8,128)S(1)} %reduce_sum.38, f32[256,512]{1,0:T(8,128)S(1)} %fusion.7), kind=kOutput, calls=%fused_computation.1 | convolution fusion | flops 1611137024 | bytes 5767172 | tf_op jit(solution)/shard_map/dot_general | solution.py:32
  101.9 6.5 %dynamic_update_slice.7 = f32[4608,512]{1,0:T(8,128)} dynamic-update-slice(f32[4608,512]{1,0:T(8,128)} %dynamic_update_slice.6, f32[1024,512]{1,0:T(8,128)S(1)} %dynamic-slice_subtract_fusion, s32[]{:T(128)S(6)} %select_n.99, s32[]{:T(128)} %constant.9.clone.1) | dynamic-update-slice | bytes 4194308 | tf_op jit(solution)/shard_map/dynamic_update_slice | solution.py:51
  108.4 1.3 slice.16
  109.7 1.9 %collective-permute-start.1 = (f32[512,512]{1,0:T(8,128)S(1)}, f32[512,512]{1,0:T(8,128)S(1)}, u32[]{:S(2)}, u32[]{:S(2)}) collective-permute-start(f32[512,512]{1,0:T(8,128)S(1)} %slice.16), channel_id=1, source_target_pairs={{0,2},{2,4},{4,6},{6,8},{8,10},{10,12},{12,14},{14,16},{16,18},{18... | collective-permute-start | bytes 3145736 | tf_op jit(solution)/shard_map/ppermute | solution.py:18
  111.6 3.9 %slice.18 = f32[3584,512]{1,0:T(8,128)S(1)} slice(f32[4608,512]{1,0:T(8,128)} %dynamic_update_slice.7), slice={[512:4096], [0:512]} | slice | bytes 14680064 | tf_op jit(solution)/shard_map/slice | solution.py:54
  115.6 11.2 %collective-permute-done.1 = f32[512,512]{1,0:T(8,128)S(1)} collective-permute-done((f32[512,512]{1,0:T(8,128)S(1)}, f32[512,512]{1,0:T(8,128)S(1)}, u32[]{:S(2)}, u32[]{:S(2)}) %collective-permute-start.1) | collective-permute-done | bytes 1048608 | tf_op jit(solution)/shard_map/ppermute | solution.py:18
  126.7 1.4 %slice_select_fusion = f32[512,512]{1,0:T(8,128)S(1)} fusion(f32[512,512]{1,0:T(8,128)S(1)} %collective-permute-done.1, f32[4608,512]{1,0:T(8,128)} %dynamic_update_slice.7, pred[]{:T(512)S(6)} %gt.3), kind=kLoop, calls=%fused_computation.7 | loop fusion | flops 262144 | bytes 3145729 | tf_op jit(solution)/shard_map/jit(_where)/select_n | solution.py:53
  128.1 4.4 %pad_maximum_fusion = f32[4096,512]{1,0:T(8,128)} fusion(f32[3584,512]{1,0:T(8,128)S(1)} %slice.18, f32[512,512]{1,0:T(8,128)S(1)} %slice_select_fusion), kind=kLoop, calls=%fused_computation | loop fusion | flops 2097152 | bytes 16777216 | tf_op jit(solution)/shard_map/concatenate | solution.py:54
  (10 shorter events, 1.4 us)
Async XLA Ops:
  6.5 52.3 %all-gather.7.cloned.1.call-start = ((), (), s32[]{:S(2)}) async-start(), calls=%async_computation | async-start | bytes 3145728 | tf_op jit(solution)/shard_map/all_gather | solution.py:12
  12.0 80.2 %all-gather.9.cloned.1.call-start = ((), (), s32[]{:S(2)}) async-start(), calls=%async_computation.1 | async-start | bytes 3145728 | tf_op jit(solution)/shard_map/all_gather | solution.py:12
  13.3 44.3 %collective-permute-start = (f32[512,512]{1,0:T(8,128)S(1)}, f32[512,512]{1,0:T(8,128)S(1)}, u32[]{:S(2)}, u32[]{:S(2)}) collective-permute-start(f32[512,512]{1,0:T(8,128)S(1)} %slice.12), channel_id=1, source_target_pairs={{2,0},{4,2},{6,4},{8,6},{10,8},{12,10},{14,12},{16,14},{18,16},{20... | collective-permute-start | bytes 3145736 | tf_op jit(solution)/shard_map/ppermute | solution.py:18
  109.7 17.0 %collective-permute-start.1 = (f32[512,512]{1,0:T(8,128)S(1)}, f32[512,512]{1,0:T(8,128)S(1)}, u32[]{:S(2)}, u32[]{:S(2)}) collective-permute-start(f32[512,512]{1,0:T(8,128)S(1)} %slice.16), channel_id=1, source_target_pairs={{0,2},{2,4},{4,6},{6,8},{8,10},{10,12},{12,14},{14,16},{16,18},{18... | collective-permute-start | bytes 3145736 | tf_op jit(solution)/shard_map/ppermute | solution.py:18
Sparse Core Ops, SparseCore 0:
  12.1 44.3 all-gather.6
  58.0 34.1 all-gather.8
